TPU v7x, 16 devices: a whole 2x2x2 slice. The times are simulated.
16 devices in a mesh: data: 16 (over z, y, x, core).
Axes of the slice: x: 2, y: 2, z: 2, core: 2. Of those that a mesh axis runs over, the one named last changes fastest.
Arguments:
- tokens: bfloat16 [8192, 1024], P('data')
- labels: int32 [2, 8192], P(None, 'data')
- w_one: bfloat16 [1024, 4096], replicated
- w_two: bfloat16 [4096, 1024], replicated
- adapter_a: bfloat16 [1024, 16], replicated
- adapter_b: bfloat16 [16, 4096], replicated
- task_heads: bfloat16 [2, 1024, 19], replicated
Outputs:
- output 1: float32 [2], replicated
- output 2: float32 [1024, 16], P('data')
- output 3: float32 [16, 4096], P(None, 'data')
All inputs are finite; a program needn't handle non-finite values.
Results may differ from a plain program's by a relative error of at most 0.00221719.
Values are sent between devices in bfloat16 or wider.
A program may use at most 1 GiB of HBM per device.

v0:
```python
import jax
import jax.numpy as jnp
from jax import lax
from jax.sharding import PartitionSpec as P

EG_STEPS = 20


def weight_solver(gram_mat):
    num_tasks = gram_mat.shape[0]
    eg_scale = jnp.trace(gram_mat) / num_tasks

    def eg_step(step_idx, weights):
        weights = weights * jnp.exp(-jnp.sum(gram_mat * weights[None, :], axis=1) / eg_scale)
        return weights / jnp.sum(weights)

    return lax.fori_loop(0, EG_STEPS, eg_step, jnp.full((num_tasks,), 1.0 / num_tasks, jnp.float32))


def task_grads(tokens, labels, w_one, w_two, adapter_a, adapter_b, task_heads):
    num_classes = task_heads.shape[2]
    low_rank = jnp.dot(tokens, adapter_a, preferred_element_type=jnp.float32).astype(jnp.bfloat16)
    pre_act = jnp.dot(tokens, w_one, preferred_element_type=jnp.float32) + jnp.dot(low_rank, adapter_b, preferred_element_type=jnp.float32)
    gelu_out, gelu_slope = jax.jvp(jax.nn.gelu, (pre_act,), (jnp.ones_like(pre_act),))
    hidden = gelu_out.astype(jnp.bfloat16)
    trunk_out = (tokens.astype(jnp.float32) + jnp.dot(hidden, w_two, preferred_element_type=jnp.float32)).astype(jnp.bfloat16)
    logits = jnp.einsum("bd,tdc->tbc", trunk_out, task_heads, preferred_element_type=jnp.float32)
    task_probs = jax.nn.softmax(logits, axis=-1)
    onehot = (labels[:, :, None] == jnp.arange(num_classes)[None, None, :]).astype(jnp.float32)
    logit_err = (task_probs - onehot).astype(jnp.bfloat16)
    d_trunk = jnp.einsum("tbc,tdc->tbd", logit_err, task_heads, preferred_element_type=jnp.float32).astype(jnp.bfloat16)
    d_hidden = jnp.einsum("tbd,fd->tbf", d_trunk, w_two, preferred_element_type=jnp.float32)
    d_pre = (d_hidden * gelu_slope[None]).astype(jnp.bfloat16)
    part_b = jnp.einsum("cs,ucg->usg", low_rank, d_pre, preferred_element_type=jnp.float32)
    d_low = jnp.einsum("tbf,rf->tbr", d_pre, adapter_b, preferred_element_type=jnp.float32).astype(jnp.bfloat16)
    part_a = jnp.einsum("bd,tbr->tdr", tokens, d_low, preferred_element_type=jnp.float32)
    return part_a, part_b


def solution(mesh):
    num_dev = mesh.shape["data"]

    def device_step(tokens, labels, w_one, w_two, adapter_a, adapter_b, task_heads):
        batch_total = tokens.shape[0] * num_dev
        part_a, part_b = task_grads(tokens, labels, w_one, w_two, adapter_a, adapter_b, task_heads)
        shard_a = lax.psum_scatter(part_a, "data", scatter_dimension=1, tiled=True) / batch_total
        shard_b = lax.psum_scatter(part_b, "data", scatter_dimension=2, tiled=True) / batch_total
        gram_part = jnp.einsum("tdr,sdr->ts", shard_a, shard_a, precision=lax.Precision.HIGHEST) + jnp.einsum("usg,tsg->ut", shard_b, shard_b, precision=lax.Precision.HIGHEST)
        gram_mat = lax.psum(gram_part, "data")
        task_weights = weight_solver(gram_mat)
        comb_a = jnp.sum(task_weights[:, None, None] * shard_a, axis=0)
        comb_b = jnp.sum(task_weights[:, None, None] * shard_b, axis=0)
        return task_weights, comb_a, comb_b

    return jax.shard_map(device_step, mesh=mesh, in_specs=(P("data", None), P(None, "data"), P(), P(), P(), P(), P()), out_specs=(P(), P("data", None), P(None, "data")), check_vma=False)
```

profile of v0, /device:TPU:0, one launch (start us, length us, event | category | flops | bytes accessed | tf_op | source)
XLA Modules:
  0.0 243.0 jit_solution(941721305719208498)
XLA Ops:
  7.2 1.6 convolution_convert_fusion.1
  8.9 7.2 %fusion.44 = f32[512,4096]{1,0:T(8,128)S(1)} fusion(bf16[512,1024]{1,0:T(8,128)(2,1)} %param.9, bf16[1024,4096]{1,0:T(8,128)(2,1)} %param.11), kind=kOutput, calls=%fused_computation.60 | convolution fusion | flops 4294967296 | bytes 17825792 | tf_op jit(solution)/shard_map/dot_general | solution.py:23
  16.1 8.6 %fusion.10 = (f32[512,4096]{1,0:T(8,128)}, f32[512,4096]{1,0:T(8,128)}) fusion(f32[512,4096]{1,0:T(8,128)S(1)} %fusion.44, bf16[512,16]{0,1:T(8,128)(2,1)S(1)} %convolution_convert_fusion.1, bf16[16,4096]{1,0:T(8,128)(2,1)S(1)} %copy-done), kind=kOutput, calls=%fused_computation.17 | convolution fusion | flops 102760448 | bytes 25313280 | tf_op jit(solution)/shard_map/dot_general | solution.py:23
  24.7 11.2 %convolution_bitcast_fusion.2 = f32[2,512,19]{1,2,0:T(8,128)S(1)} fusion(bf16[4096,1024]{1,0:T(8,128)(2,1)} %param.12, f32[512,4096]{1,0:T(8,128)} %get-tuple-element.52, bf16[512,1024]{1,0:T(8,128)(2,1)S(1)} %copy-done.1, bf16[2,1024,19]{1,0,2:T(2,128)(2,1)S(1)} %copy-done.3), kind=kOutput, calls=%fused_computation.30 | convolution fusion | flops 4355260416 | bytes 17981440 | tf_op jit(solution)/shard_map/bd,tdc->tbc/dot_general | solution.py:27
  36.2 15.9 %multiply_convert_fusion = bf16[2,512,4096]{2,1,0:T(8,128)(2,1)} fusion(bf16[4096,1024]{1,0:T(8,128)(2,1)} %param.12, f32[512,4096]{1,0:T(8,128)} %get-tuple-element.51, bf16[2,1024,19]{1,0,2:T(2,128)(2,1)S(1)} %copy-done.3, f32[2,512,19]{1,2,0:T(8,128)S(1)} %get-tuple-element.54, s32[2,512]{1,0:T(2,128)S(1)} %copy-done.4, f32[2,512]{1,0:T(2,128)S(1)} %get-tuple-element.53), kind=kOutput, calls=%fused_computation.5 | convolution fusion | flops 8639314944 | bytes 25329664 | tf_op jit(solution)/shard_map/tbd,fd->tbf/dot_general | solution.py:32
  52.0 5.9 %convolution_bitcast_fusion.1 = f32[2,1024,16]{1,2,0:T(8,128)S(1)} fusion(bf16[2,512,4096]{2,1,0:T(8,128)(2,1)} %multiply_convert_fusion, bf16[512,1024]{1,0:T(8,128)(2,1)S(1)} %copy-done.1, bf16[16,4096]{1,0:T(8,128)(2,1)S(1)} %copy-done), kind=kOutput, calls=%fused_computation.28 | convolution fusion | flops 167788544 | bytes 9699328 | tf_op jit(solution)/shard_map/bd,tbr->tdr/dot_general | solution.py:36
  58.4 1.5 reshape.19
  60.0 5.4 %convolution_bitcast_fusion = f32[2,16,4096]{2,1,0:T(8,128)} fusion(bf16[2,512,4096]{2,1,0:T(8,128)(2,1)} %multiply_convert_fusion, bf16[512,16]{0,1:T(8,128)(2,1)S(1)} %convolution_convert_fusion.1), kind=kOutput, calls=%fused_computation.21 | convolution fusion | flops 134217728 | bytes 8929280 | tf_op jit(solution)/shard_map/cs,ucg->usg/dot_general | solution.py:34
  65.4 52.0 %reduce-scatter.7.cloned.1.call-done = f32[64,32]{1,0:T(8,128)} async-done(((f32[1024,32]{1,0:T(8,128)}), f32[64,32]{1,0:T(8,128)}) %reduce-scatter.7.cloned.1.call-update) | async-done | bytes 8208
  117.4 0.9 reshape.20
  118.4 53.9 %reduce-scatter.5.cloned.1.call-done = f32[2,16,256]{2,1,0:T(8,128)} async-done(((f32[2,16,4096]{2,1,0:T(8,128)}), f32[2,16,256]{2,1,0:T(8,128)}) %reduce-scatter.5.cloned.1.call-update) | async-done | bytes 32784 | tf_op jit(solution)/shard_map/reduce_scatter | solution.py:47
  172.3 0.8 broadcast_multiply_fusion
  173.7 30.8 %psum.7 = f32[2,2]{1,0:T(2,128)S(1)} all-reduce(f32[2,2]{1,0:T(2,128)S(1)} %fusion.19), channel_id=1, replica_groups=mesh['data'=16] {'data'}, use_global_device_ids=true, to_apply=%region_4.0 | all-reduce | flops 4 | bytes 32 | tf_op jit(solution)/shard_map/psum | solution.py:49
  205.7 28.4 %while.11 = (s32[]{:T(128)}, f32[2]{0:T(128)S(1)}, f32[2,2]{1,0:T(2,128)S(1)}, f32[]{:T(128)}, s32[]{:T(128)}, /*index=5*/s32[]{:T(128)}) while((s32[]{:T(128)}, f32[2]{0:T(128)S(1)}, f32[2,2]{1,0:T(2,128)S(1)}, f32[]{:T(128)}, s32[]{:T(128)}, /*index=5*/s32[]{:T(128)}) %tuple.31), condition=%wide.region_9.10_spmd.clone, body=%wide.region_6.9_spmd.clone.sunk | while | flops 22 | bytes 180 | solution.py:17
  206.4 0.6 broadcast_divide_fusion.2
  207.9 0.6 broadcast_divide_fusion.2
  210.7 0.6 broadcast_divide_fusion.2
  212.1 0.6 broadcast_divide_fusion.2
  215.0 0.6 broadcast_divide_fusion.2
  216.4 0.6 broadcast_divide_fusion.2
  219.2 0.6 broadcast_divide_fusion.2
  220.6 0.6 broadcast_divide_fusion.2
  234.1 0.7 multiply_reduce_fusion.2
  234.8 1.4 multiply_reduce_fusion.1
  (95 shorter events, 24.8 us)
Async XLA Ops:
  7.2 8.9 %copy-start = (bf16[16,4096]{1,0:T(8,128)(2,1)S(1)}, bf16[16,4096]{1,0:T(8,128)(2,1)}, u32[]{:S(2)}) copy-start(bf16[16,4096]{1,0:T(8,128)(2,1)} %param.14) | copy-start | bytes 393220
  7.2 110.2 %reduce-scatter.7.cloned.1.call-start = ((), (), s32[]{:S(2)}) async-start(), calls=%async_computation.3 | async-start | bytes 557056
  16.1 8.6 %copy-start.1 = (bf16[512,1024]{1,0:T(8,128)(2,1)S(1)}, bf16[512,1024]{1,0:T(8,128)(2,1)}, u32[]{:S(2)}) copy-start(bf16[512,1024]{1,0:T(8,128)(2,1)} %param.9) | copy-start | bytes 3145732
  16.1 8.6 %copy-start.3 = (bf16[2,1024,19]{1,0,2:T(2,128)(2,1)S(1)}, bf16[2,1024,19]{1,0,2:T(2,128)(2,1)}, u32[]{:S(2)}) copy-start(bf16[2,1024,19]{1,0,2:T(2,128)(2,1)} %param.15) | copy-start | bytes 233476
  24.7 11.5 %copy-start.4 = (s32[2,512]{1,0:T(2,128)S(1)}, s32[2,512]{1,0:T(2,128)}, u32[]{:S(2)}) copy-start(s32[2,512]{1,0:T(2,128)} %param.10) | copy-start | bytes 12292
  59.9 112.3 %reduce-scatter.5.cloned.1.call-start = ((), (), s32[]{:S(2)}) async-start(), calls=%async_computation.2 | async-start | bytes 557056 | tf_op jit(solution)/shard_map/reduce_scatter | solution.py:47
  234.1 2.1 copy-start.2
Sparse Core Ops, SparseCore 0:
  60.0 57.3 reduce-scatter.6
  119.6 52.5 reduce-scatter.4
where the time goes:
time: 244 us; the launch traced here: 243 us
  waiting for transfers between devices  106 us (43%)
  matrix products  56.4 us (23%)
  other arithmetic  31.5 us (13%)
  blocking collectives  30.8 us (13%)
  between operations  14.8 us (6%)
  local copies, waits for them, and re-layouts  2.96 us (1%)
    reduce_scatter x1, waiting for transfers between devices, device_step(): lax.psum_scatter(part_b, 'data', scatter_dimension=2, tiled=True)  53.9 us
    unnamed x3, waiting for transfers between devices  52 us
    psum x1, blocking collectives, device_step(): gram_mat = lax.psum(gram_part, 'data')  30.8 us
    dot_general x1, matrix products, task_grads(): jnp.einsum('tbd,fd->tbf', d_trunk, w_two, preferred_element_type=jnp.floa...  15.9 us
    div x20, other arithmetic, eg_step(): return weights / jnp.sum(weights)  13 us
    reduce_sum x20, other arithmetic, eg_step(): return weights / jnp.sum(weights)  12.4 us
    dot_general x1, matrix products, task_grads(): jnp.einsum('bd,tdc->tbc', trunk_out, task_heads, preferred_element_type=j...  11.2 us
    dot_general x1, matrix products, task_grads(): jnp.dot(low_rank, adapter_b, preferred_element_type=jnp.float32)  8.57 us
  transfers between devices with their start and end apart: 2, of which 2 were waited for; matrix products, arithmetic and copies ran while one was open for 3% of the time, Pallas kernels for 0%

commit v1 on v0

v1 whole, which is shorter than its diff:
```python
import functools

import jax
import jax.numpy as jnp
from jax import lax
from jax.experimental import pallas as pl
from jax.experimental.pallas import tpu as pltpu
from jax.sharding import PartitionSpec as P

EG_STEPS = 20
BF = jnp.bfloat16
F32 = jnp.float32
GELU_C = 0.7978845608028654
GELU_A = 0.044715
MESH = pl.DeviceIdType.MESH
BITS = (1, 2, 4, 8)
NT = (((1,), (1,)), ((), ()))
TN = (((0,), (0,)), ((), ()))


def xor(a, b):
    return sum(bit * ((a // bit + b // bit) % 2) for bit in BITS)


def mm(a, b, dims=(((1,), (0,)), ((), ()))):
    return lax.dot_general(a, b, dims, preferred_element_type=F32)


def kernel(cfg, x_hbm, lab_hbm, w1_hbm, w2_hbm, a_hbm, b_hbm, head_hbm, alpha_ref, ga_ref, gb_ref, xu, w1b, w2, a_v, head_v, lab_v, head_t, u_t, p0, p1, act, slope, z, dz, dp0, dp1, du_t, send_b, recv_b, send_a, recv_a, send_m, recv_m, load_sem, sb_sem, rb_sem, sa_sem, ra_sem, sm_sem, rm_sem):
    n_dev, total = cfg
    tok, d_model = x_hbm.shape
    d_ff = w1_hbm.shape[1]
    rank = a_hbm.shape[0]
    n_cls = head_hbm.shape[0]
    col = d_ff // n_dev
    fc = 2 * col
    n_ch = n_dev // 2
    zc = d_model // 4
    me = lax.axis_index("data")
    chip, core = me // 2, me % 2

    barrier = pltpu.get_barrier_semaphore()
    for k in range(1, n_dev):
        pl.semaphore_signal(barrier, inc=1, device_id=(xor(me, k),), device_id_type=MESH)

    def w1_load(i):
        cols = pl.ds(pl.multiple_of(i * fc, fc), fc)
        return pltpu.make_async_copy(w1_hbm.at[:, cols], w1b.at[pl.ds(0, d_model), cols], load_sem.at[i])

    def w2_load(i):
        cols = pl.ds(pl.multiple_of(i * zc, zc), zc)
        return pltpu.make_async_copy(w2_hbm.at[:, cols], w2.at[:, cols], load_sem.at[n_ch + i])

    base = n_ch + 4
    load_x = pltpu.make_async_copy(x_hbm, xu.at[:, pl.ds(0, d_model)], load_sem.at[base])
    load_a = pltpu.make_async_copy(a_hbm, a_v, load_sem.at[base + 1])
    load_b = pltpu.make_async_copy(b_hbm, w1b.at[pl.ds(d_model, rank), :], load_sem.at[base + 2])
    load_h = pltpu.make_async_copy(head_hbm, head_v, load_sem.at[base + 3])
    load_l = pltpu.make_async_copy(lab_hbm, lab_v, load_sem.at[base + 4])
    load_x.start()
    load_a.start()
    w1_load(0).start()
    load_b.start()
    w1_load(1).start()
    load_h.start()
    load_l.start()
    for i in range(2, n_ch):
        w1_load(i).start()
    for i in range(4):
        w2_load(i).start()

    pad = xu.shape[1] - d_model
    xu[:, d_model:] = jnp.zeros((tok, pad), BF)
    w1b[d_model + rank:, :] = jnp.zeros((pad - rank, d_ff), BF)
    du_t[...] = jnp.zeros_like(du_t)
    load_x.wait()
    load_a.wait()
    low = mm(xu[:, :d_model], a_v[...], NT)
    xu[:, d_model:d_model + rank] = low.astype(BF)
    u_t[...] = low.T.astype(BF)

    def pre(i, p_ref):
        w1_load(i).wait()
        p_ref[...] = mm(xu[...], w1b[:, pl.ds(pl.multiple_of(i * fc, fc), fc)])

    def gelu(i, p_ref):
        x = p_ref[...]
        x2 = x * x
        t = jnp.tanh(x * (GELU_C + (GELU_C * GELU_A) * x2))
        hx = 0.5 * x
        t1 = 1.0 + t
        act[:, pl.ds(pl.multiple_of(i * fc, fc), fc)] = (hx * t1).astype(BF)
        slope[i] = 0.5 * t1 + (hx * (1.0 - t * t)) * (GELU_C + (3.0 * GELU_C * GELU_A) * x2)

    load_b.wait()
    pre(0, p0)

    def fwd(j, _):
        pre(2 * j + 1, p1)
        gelu(2 * j, p0)
        pre(2 * j + 2, p0)
        gelu(2 * j + 1, p1)
        return 0

    lax.fori_loop(0, n_ch // 2 - 1, fwd, 0)
    pre(n_ch - 1, p1)
    gelu(n_ch - 2, p0)

    load_h.wait()
    load_l.wait()
    head_t[...] = jnp.zeros_like(head_t)
    for t in range(2):
        head_t[32 * t:32 * t + n_cls, :] = head_v[:, t, :]
    gelu(n_ch - 1, p1)

    def out_block(i, _):
        w2_load(i).wait()
        cols = pl.ds(pl.multiple_of(i * zc, zc), zc)
        z[:, cols] = (xu[:, cols].astype(F32) + mm(act[...], w2[:, cols])).astype(BF)
        return 0

    lax.fori_loop(0, 4, out_block, 0)

    logits = mm(head_t[...], z[...], NT)
    rows = lax.broadcasted_iota(jnp.int32, (32, tok), 0)
    for t in range(2):
        lg = jnp.where(rows < n_cls, logits[32 * t:32 * t + 32], -jnp.inf)
        ex = jnp.exp(lg - jnp.max(lg, axis=0, keepdims=True))
        prob = ex / jnp.sum(ex, axis=0, keepdims=True)
        err = (prob - (rows == lab_v[t:t + 1, :]).astype(F32)).astype(BF)
        dz[tok * t:tok * t + tok, :] = mm(err, head_t[32 * t:32 * t + 32, :], TN).astype(BF)

    pl.semaphore_wait(barrier, n_dev - 1)

    def chunk_of(kk):
        return xor(chip, kk)

    def d_pre(kk, dp_ref):
        c = chunk_of(kk)
        dh = mm(dz[...], w2[pl.ds(pl.multiple_of(c * fc, fc), fc), :], NT)
        sl = slope[c]
        for t in range(2):
            dp_ref[tok * t:tok * t + tok, :] = (dh[tok * t:tok * t + tok] * sl).astype(BF)

    def b_copy(kk, half):
        dst_core = half
        k = 2 * kk + (core + half) % 2
        return pltpu.make_async_remote_copy(
            src_ref=send_b.at[kk, half], dst_ref=recv_b.at[k], send_sem=sb_sem.at[k], recv_sem=rb_sem.at[k],
            device_id=(2 * chunk_of(kk) + dst_core,), device_id_type=MESH)

    def grads(kk, dp_ref):
        c = chunk_of(kk)
        for t in range(2):
            gb = mm(u_t[...], dp_ref[tok * t:tok * t + tok, :])
            for half in range(2):
                send_b[kk, half, t] = gb[:, col * half:col * half + col]
        bm = w1b[pl.ds(d_model, rank), pl.ds(pl.multiple_of(c * fc, fc), fc)]
        du_t[...] += mm(bm, dp_ref[...], NT)

    d_pre(n_ch - 1, dp0)

    def bwd(j, _):
        kk = n_ch - 1 - 2 * j
        d_pre(kk - 1, dp1)
        grads(kk, dp0)
        b_copy(kk, 0).start()
        b_copy(kk, 1).start()
        d_pre(kk - 2, dp0)
        grads(kk - 1, dp1)
        b_copy(kk - 1, 0).start()
        b_copy(kk - 1, 1).start()
        return 0

    lax.fori_loop(0, n_ch // 2 - 1, bwd, 0)
    d_pre(0, dp1)
    grads(1, dp0)
    b_copy(1, 0).start()
    b_copy(1, 1).start()
    grads(0, dp1)
    b_copy(0, 1 - core).start()

    lane = lax.broadcasted_iota(jnp.int32, (rank, 128), 1)
    ga = [mm(du_t[:, tok * t:tok * t + tok].astype(BF), xu[:, :d_model]) for t in range(2)]
    for j in range(n_ch):
        a0, a1 = (ga[t][:, 128 * j:128 * j + 128] for t in range(2))
        send_a[2 * j] = jnp.where(lane < 64, a0, pltpu.roll(a1, 64, 1))
        send_a[2 * j + 1] = jnp.where(lane < 64, pltpu.roll(a0, 64, 1), a1)

    def a_copy(k):
        dst = xor(me, k)
        return pltpu.make_async_remote_copy(
            src_ref=send_a.at[dst], dst_ref=recv_a.at[k], send_sem=sa_sem.at[k], recv_sem=ra_sem.at[k],
            device_id=(dst,), device_id_type=MESH)

    def m_copy(k):
        return pltpu.make_async_remote_copy(
            src_ref=send_m, dst_ref=recv_m.at[k], send_sem=sm_sem.at[k], recv_sem=rm_sem.at[k],
            device_id=(xor(me, k),), device_id_type=MESH)

    order = [15, 14, 13, 11, 10, 7, 6, 12, 9, 5, 3, 8, 4, 2, 1]
    for k in order:
        a_copy(k).start()

    def b_half(k):
        return b_copy(k // 2, (core + k) % 2)

    sum_b = send_b[0, core]
    for k in reversed(range(1, n_dev)):
        b_half(k).wait_recv()
        sum_b = sum_b + recv_b[k]
    sum_b = sum_b * (1.0 / total)
    b0, b1 = sum_b[0], sum_b[1]
    sq0, sq1, cross = b0 * b0, b1 * b1, b0 * b1
    sum_a = send_a[me]
    for k in reversed(order):
        a_copy(k).wait_recv()
        sum_a = sum_a + recv_a[k]
    sum_a = sum_a * (1.0 / total)
    sq = sum_a * sum_a
    sign = jnp.where(lane < 64, 1.0, -1.0)
    other = pltpu.roll(sum_a, 64, 1)

    def fold(part_b, part_a):
        return jnp.sum(part_b[:, :128] + part_b[:, 128:] + part_a, axis=0, keepdims=True)

    diff = fold(sq0 - sq1, sq * sign)
    both = fold(sq0 + sq1, sq)
    mix = fold(cross, 0.5 * sum_a * other)
    send_m[0:1, :] = diff
    send_m[1:2, :] = both
    send_m[2:3, :] = mix
    send_m[3:4, :] = jnp.zeros_like(mix)
    for k in order:
        m_copy(k).start()
    sum_m = send_m[...]
    for k in reversed(order):
        m_copy(k).wait_recv()
        sum_m = sum_m + recv_m[k]
    gram = jnp.broadcast_to(jnp.sum(sum_m, axis=1, keepdims=True), sum_m.shape)
    m_diff, m_both, m_mix = gram[0:1], gram[1:2], gram[2:3]
    scale = 0.5 / m_both
    c0 = m_diff * scale
    c1 = (m_both - 2.0 * m_mix) * scale
    e = jnp.zeros_like(c0)
    for _ in range(EG_STEPS):
        e = e - (c0 + c1 * jnp.tanh(e))
    al0 = 1.0 / (1.0 + jnp.exp(-2.0 * e))
    al1 = 1.0 / (1.0 + jnp.exp(2.0 * e))
    gb_ref[...] = al0[:, 0:1] * b0 + al1[:, 0:1] * b1
    ga_ref[...] = (al0 * sum_a + al1 * other)[:, :64]
    alpha_ref[...] = jnp.where(lane[0:1, :] == 0, al0, al1)[:, 0:2]
    for k in range(1, n_dev):
        b_half(k).wait_send()
        a_copy(k).wait_send()
        m_copy(k).wait_send()


def solution(mesh):
    n_dev = mesh.shape["data"]

    def device_step(tokens, labels, w_one, w_two, adapter_a, adapter_b, task_heads):
        tok, d_model = tokens.shape
        d_ff = w_one.shape[1]
        rank = adapter_a.shape[1]
        n_tasks, _, n_cls = task_heads.shape
        col = d_ff // n_dev
        fc = 2 * col
        dma = pltpu.SemaphoreType.DMA
        alpha, ga, gb = pl.pallas_call(
            functools.partial(kernel, (n_dev, tok * n_dev)),
            out_shape=(
                jax.ShapeDtypeStruct((1, n_tasks), F32),
                jax.ShapeDtypeStruct((rank, d_model // n_dev), F32),
                jax.ShapeDtypeStruct((rank, col), F32),
            ),
            in_specs=[pl.BlockSpec(memory_space=pl.ANY)] * 7,
            out_specs=[pl.BlockSpec(memory_space=pltpu.VMEM)] * 3,
            scratch_shapes=[
                pltpu.VMEM((tok, d_model + 128), BF),
                pltpu.VMEM((d_model + 128, d_ff), BF),
                pltpu.VMEM((d_ff, d_model), BF),
                pltpu.VMEM((rank, d_model), BF),
                pltpu.VMEM((n_cls, n_tasks, d_model), BF),
                pltpu.VMEM((n_tasks, tok), jnp.int32),
                pltpu.VMEM((n_tasks * 32, d_model), BF),
                pltpu.VMEM((rank, tok), BF),
                pltpu.VMEM((tok, fc), F32),
                pltpu.VMEM((tok, fc), F32),
                pltpu.VMEM((tok, d_ff), BF),
                pltpu.VMEM((n_dev // 2, tok, fc), F32),
                pltpu.VMEM((tok, d_model), BF),
                pltpu.VMEM((n_tasks * tok, d_model), BF),
                pltpu.VMEM((n_tasks * tok, fc), BF),
                pltpu.VMEM((n_tasks * tok, fc), BF),
                pltpu.VMEM((rank, n_tasks * tok), F32),
                pltpu.VMEM((n_dev // 2, 2, n_tasks, rank, col), F32),
                pltpu.VMEM((n_dev, n_tasks, rank, col), F32),
                pltpu.VMEM((n_dev, rank, 128), F32),
                pltpu.VMEM((n_dev, rank, 128), F32),
                pltpu.VMEM((4, 128), F32),
                pltpu.VMEM((n_dev, 4, 128), F32),
                dma((n_dev // 2 + 9,)),
                dma((n_dev,)), dma((n_dev,)), dma((n_dev,)), dma((n_dev,)), dma((n_dev,)), dma((n_dev,)),
            ],
            compiler_params=pltpu.CompilerParams(collective_id=0, has_side_effects=True, vmem_limit_bytes=60 * 1024 * 1024),
            name="step",
        )(tokens, labels, w_one, w_two, adapter_a.T, adapter_b, task_heads.transpose(2, 0, 1))
        return alpha.reshape(n_tasks), ga.T, gb

    return jax.shard_map(device_step, mesh=mesh, in_specs=(P("data", None), P(None, "data"), P(), P(), P(), P(), P()), out_specs=(P(), P("data", None), P(None, "data")), check_vma=False)
```

time: 244 us -> 54.4 us (0.22)
  waiting for transfers between devices: 106 us -> 0 us
  matrix products: 56.4 us -> 0 us
  Pallas kernels: 0 us -> 49.7 us
  other arithmetic: 31.5 us -> 0 us
  blocking collectives: 30.8 us -> 0 us
  between operations: 14.8 us -> 0.64 us
    dot_general x9 -> x0, matrix products: 56.4 us -> none  [the longest x1 15.9 us: task_grads(): jnp.einsum('tbd,fd->tbf', d_trunk, w_two, preferred_element_type=jnp.floa...]
    reduce_scatter x1 -> x0, waiting for transfers between devices: 53.9 us -> none  [device_step(): lax.psum_scatter(part_b, 'data', scatter_dimension=2, tiled=True)]
    unnamed x3 -> x0, waiting for transfers between devices: 52 us -> none
    pallas_call x0 -> x1, Pallas kernels: none -> 49.7 us  [device_step(): pl.pallas_call(functools.partial(kernel, (n_dev, tok * n_dev)), out_shape...]
    psum x1 -> x0, blocking collectives: 30.8 us -> none  [device_step(): gram_mat = lax.psum(gram_part, 'data')]
    reduce_sum x43 -> x0, other arithmetic: 17.4 us -> none  [the longest x20 12.4 us: eg_step(): return weights / jnp.sum(weights)]
    div x22 -> x0, other arithmetic: 13.7 us -> none  [the longest x20 13 us: eg_step(): return weights / jnp.sum(weights)]
  transfers between devices with their start and end apart: 2 -> 0, of which waited for: 2 -> 0; matrix products, arithmetic and copies ran while one was open for 3% -> 0% of each run, Pallas kernels for 0% -> 0%
where the time goes in v1:
time: 54.4 us; the launch traced here: 54.1 us
  Pallas kernels  49.7 us (91%)
  local copies, waits for them, and re-layouts  3.8 us (7%)
  between operations  0.64 us (1%)
    pallas_call x1, Pallas kernels, device_step(): pl.pallas_call(functools.partial(kernel, (n_dev, tok * n_dev)), out_shape...  49.7 us
    unnamed x3, local copies, waits for them, and re-layouts  3.8 us

profile of v1, /device:TPU:0, one launch (start us, length us, event | category | flops | bytes accessed | tf_op | source)
XLA Modules:
  0.0 54.1 jit_solution(15185603015797531881)
XLA Ops:
  0.6 49.7 %step.1 = (f32[1,2]{1,0:T(1,128)}, f32[16,64]{1,0:T(8,128)}, f32[16,256]{1,0:T(8,128)}) custom-call(bf16[512,1024]{1,0:T(8,128)(2,1)} %x_hbm.1, s32[2,512]{1,0:T(2,128)} %lab_hbm.1, bf16[1024,4096]{1,0:T(8,128)(2,1)} %w1_hbm.1, bf16[4096,1024]{1,0:T(8,128)(2,1)} %w2_hbm.1, bf16[16,1024]{1,0:T(8,128)(2,1)} %bitcast.5, bf16[16,4096]{1,0:T(8,128)(2,1)} %b_hbm.1, ...), custom_call_target="tpu_custom_call" | custom-call | tf_op jit(solution)/shard_map/step/pallas_call | solution.py:270
  50.3 1.2 %copy.13 = f32[2]{0:T(128)} copy(f32[2]{0:T(128)} %bitcast.7) | data formatting | bytes 16
  51.5 1.3 %copy.14 = f32[64,16]{0,1:T(8,128)} copy(f32[64,16]{0,1:T(8,128)} %bitcast.6) | data formatting | bytes 8192
  52.8 1.3 %copy.15 = f32[16,256]{1,0:T(8,128)} copy(f32[16,256]{1,0:T(8,128)} %get-tuple-element.14) | data formatting | bytes 32768

commit v2 on v1

--- a/solution.py
+++ b/solution.py
@@ -64,10 +64,8 @@
     w1_load(1).start()
     load_h.start()
     load_l.start()
-    for i in range(2, n_ch):
-        w1_load(i).start()
-    for i in range(4):
-        w2_load(i).start()
+    w1_load(2).start()
+    w1_load(3).start()
 
     pad = xu.shape[1] - d_model
     xu[:, d_model:] = jnp.zeros((tok, pad), BF)
@@ -79,39 +77,43 @@
     xu[:, d_model:d_model + rank] = low.astype(BF)
     u_t[...] = low.T.astype(BF)
 
-    def pre(i, p_ref):
+    def pre(i):
         w1_load(i).wait()
-        p_ref[...] = mm(xu[...], w1b[:, pl.ds(pl.multiple_of(i * fc, fc), fc)])
-
-    def gelu(i, p_ref):
-        x = p_ref[...]
-        x2 = x * x
-        t = jnp.tanh(x * (GELU_C + (GELU_C * GELU_A) * x2))
-        hx = 0.5 * x
-        t1 = 1.0 + t
-        act[:, pl.ds(pl.multiple_of(i * fc, fc), fc)] = (hx * t1).astype(BF)
-        slope[i] = 0.5 * t1 + (hx * (1.0 - t * t)) * (GELU_C + (3.0 * GELU_C * GELU_A) * x2)
+
+        @pl.when(i < n_ch // 2)
+        def _():
+            w1_load(i + n_ch // 2).start()
+
+        @pl.when(i >= n_ch // 2)
+        def _():
+            w2_load(i - n_ch // 2).start()
+
+        cols = pl.ds(pl.multiple_of(i * fc, fc), fc)
+        p = mm(xu[...], w1b[:, cols])
+        for r in range(0, tok, 16):
+            rs = pl.ds(r, 16)
+            x = p[r:r + 16]
+            x2 = x * x
+            t = jnp.tanh(x * (GELU_C + (GELU_C * GELU_A) * x2))
+            hx = 0.5 * x
+            t1 = 1.0 + t
+            act[rs, cols] = (hx * t1).astype(BF)
+            slope[i, rs, :] = 0.5 * t1 + (hx * (1.0 - t * t)) * (GELU_C + (3.0 * GELU_C * GELU_A) * x2)
 
     load_b.wait()
-    pre(0, p0)
 
     def fwd(j, _):
-        pre(2 * j + 1, p1)
-        gelu(2 * j, p0)
-        pre(2 * j + 2, p0)
-        gelu(2 * j + 1, p1)
+        pre(2 * j)
+        pre(2 * j + 1)
         return 0
 
-    lax.fori_loop(0, n_ch // 2 - 1, fwd, 0)
-    pre(n_ch - 1, p1)
-    gelu(n_ch - 2, p0)
+    lax.fori_loop(0, n_ch // 2, fwd, 0)
 
     load_h.wait()
     load_l.wait()
     head_t[...] = jnp.zeros_like(head_t)
     for t in range(2):
         head_t[32 * t:32 * t + n_cls, :] = head_v[:, t, :]
-    gelu(n_ch - 1, p1)
 
     def out_block(i, _):
         w2_load(i).wait()
@@ -254,6 +256,12 @@
         b_half(k).wait_send()
         a_copy(k).wait_send()
         m_copy(k).wait_send()
+
+
+def finish(alpha_in, ga_in, gb_in, alpha_ref, ga_ref, gb_ref):
+    alpha_ref[...] = alpha_in[...]
+    ga_ref[...] = ga_in[...]
+    gb_ref[...] = gb_in[...]
 
 
 def solution(mesh):
@@ -306,6 +314,14 @@
             compiler_params=pltpu.CompilerParams(collective_id=0, has_side_effects=True, vmem_limit_bytes=60 * 1024 * 1024),
             name="step",
         )(tokens, labels, w_one, w_two, adapter_a.T, adapter_b, task_heads.transpose(2, 0, 1))
+        outs = (alpha, ga, gb)
+        alpha, ga, gb = pl.pallas_call(
+            finish,
+            out_shape=[jax.ShapeDtypeStruct(o.shape, o.dtype) for o in outs],
+            in_specs=[pl.BlockSpec(memory_space=pltpu.VMEM)] * 3,
+            out_specs=[pl.BlockSpec(memory_space=pltpu.VMEM)] * 3,
+            name="finish",
+        )(*outs)
         return alpha.reshape(n_tasks), ga.T, gb
 
     return jax.shard_map(device_step, mesh=mesh, in_specs=(P("data", None), P(None, "data"), P(), P(), P(), P(), P()), out_specs=(P(), P("data", None), P(None, "data")), check_vma=False)

time: 54.4 us -> 46.9 us (0.86)
  local copies, waits for them, and re-layouts: 3.8 us -> 0 us
  Pallas kernels: 49.7 us -> 46.1 us
    pallas_call x1, Pallas kernels: 49.7 us -> 44.8 us  [device_step(): pl.pallas_call(functools.partial(kernel, (n_dev, tok * n_dev)), out_shape...]
    unnamed x3 -> x0, local copies, waits for them, and re-layouts: 3.8 us -> none
    pallas_call x0 -> x1, Pallas kernels: none -> 1.36 us  [device_step(): pl.pallas_call(finish, out_shape=[jax.ShapeDtypeStruct(o.shape, o.dtype)...]
where the time goes in v2:
time: 46.9 us; the launch traced here: 46.8 us
  Pallas kernels  46.1 us (98%)
  between operations  0.64 us (1%)
    pallas_call x1, Pallas kernels, device_step(): pl.pallas_call(functools.partial(kernel, (n_dev, tok * n_dev)), out_shape...  44.8 us
    pallas_call x1, Pallas kernels, device_step(): pl.pallas_call(finish, out_shape=[jax.ShapeDtypeStruct(o.shape, o.dtype)...  1.36 us

profile of v2, /device:TPU:0, one launch (start us, length us, event | category | flops | bytes accessed | tf_op | source)
XLA Modules:
  0.0 46.8 jit_solution(8917502280839182909)
XLA Ops:
  0.6 44.8 %step.1 = (f32[1,2]{1,0:T(1,128)}, f32[16,64]{1,0:T(8,128)}, f32[16,256]{1,0:T(8,128)}) custom-call(bf16[512,1024]{1,0:T(8,128)(2,1)} %x_hbm.1, s32[2,512]{1,0:T(2,128)} %lab_hbm.1, bf16[1024,4096]{1,0:T(8,128)(2,1)} %w1_hbm.1, bf16[4096,1024]{1,0:T(8,128)(2,1)} %w2_hbm.1, bf16[16,1024]{1,0:T(8,128)(2,1)} %bitcast.5, bf16[16,4096]{1,0:T(8,128)(2,1)} %b_hbm.1, ...), custom_call_target="tpu_custom_call" | custom-call | tf_op jit(solution)/shard_map/step/pallas_call | solution.py:278
  45.4 1.4 %finish.1 = (f32[1,2]{1,0:T(1,128)}, f32[16,64]{1,0:T(8,128)}, f32[16,256]{1,0:T(8,128)}) custom-call(f32[1,2]{1,0:T(1,128)} %get-tuple-element.9.alpha_in, f32[16,64]{1,0:T(8,128)} %get-tuple-element.10.ga_in, f32[16,256]{1,0:T(8,128)} %get-tuple-element.11.gb_in), custom_call_target="tpu_custom_call" | custom-call | tf_op jit(solution)/shard_map/finish/pallas_call | solution.py:318

commit v3 on v2

v3 whole, which is shorter than its diff:
```python
import functools

import jax
import jax.numpy as jnp
from jax import lax
from jax.experimental import pallas as pl
from jax.experimental.pallas import tpu as pltpu
from jax.sharding import PartitionSpec as P

EG_STEPS = 20
BF = jnp.bfloat16
F32 = jnp.float32
GELU_C = 0.7978845608028654
GELU_A = 0.044715
MESH = pl.DeviceIdType.MESH
BITS = (1, 2, 4, 8)
STRIP = 32
NT = (((1,), (1,)), ((), ()))
TN = (((0,), (0,)), ((), ()))


def xor(a, b):
    return sum(bit * ((a // bit + b // bit) % 2) for bit in BITS)


def mm(a, b, dims=(((1,), (0,)), ((), ()))):
    return lax.dot_general(a, b, dims, preferred_element_type=F32)


def kernel(cfg, x_hbm, lab_hbm, w1_hbm, w2_hbm, a_hbm, b_hbm, head_hbm, alpha_ref, ga_ref, gb_ref, xu, w1b, w2, a_v, head_v, lab_v, head_t, u_t, act, slope, z, dz, dp0, dp1, du_t, send_b, recv_b, send_a, recv_a, send_m, recv_m, load_sem, sb_sem, rb_sem, sa_sem, ra_sem, sm_sem, rm_sem):
    n_dev, total = cfg
    tok, d_model = x_hbm.shape
    d_ff = w1_hbm.shape[1]
    rank = a_hbm.shape[0]
    n_cls, n_task = head_hbm.shape[0], head_hbm.shape[1]
    col = d_ff // n_dev
    fc = 2 * col
    n_ch = n_dev // 2
    me = lax.axis_index("data")
    chip, core = me // 2, me % 2

    barrier = pltpu.get_barrier_semaphore()
    for k in range(1, n_dev):
        pl.semaphore_signal(barrier, inc=1, device_id=(xor(me, k),), device_id_type=MESH)

    sem_at = [0]

    def load(src, dst):
        copy = pltpu.make_async_copy(src, dst, load_sem.at[sem_at[0]])
        sem_at[0] += 1
        copy.start()
        return copy

    load_h = load(head_hbm, head_v)
    load_a = load(a_hbm, a_v)
    load_x = load(x_hbm, xu.at[:, pl.ds(0, d_model)])
    load_b = load(b_hbm, w1b.at[pl.ds(d_model, rank), :])
    load_w1 = [load(w1_hbm.at[:, pl.ds(i * fc, fc)], w1b.at[pl.ds(0, d_model), pl.ds(i * fc, fc)]) for i in range(n_ch)]
    load_l = load(lab_hbm, lab_v)
    w2_rows = d_ff // 4
    load_w2 = [load(w2_hbm.at[pl.ds(i * w2_rows, w2_rows), :], w2.at[pl.ds(i * w2_rows, w2_rows), :]) for i in range(4)]

    pad = xu.shape[1] - d_model
    xu[:, d_model:] = jnp.zeros((tok, pad), BF)
    w1b[d_model + rank:, :] = jnp.zeros((pad - rank, d_ff), BF)
    head_t[...] = jnp.zeros_like(head_t)
    du_t[...] = jnp.zeros_like(du_t)
    load_h.wait()
    for t in range(n_task):
        head_t[32 * t:32 * t + n_cls, :] = head_v[:, t, :]
    load_a.wait()
    load_b.wait()
    load_x.wait()
    load_w1[0].wait()
    low = mm(xu[:, :d_model], a_v[...], NT)
    xu[:, d_model:d_model + rank] = low.astype(BF)
    u_t[...] = low.T.astype(BF)

    def pre(i):
        slope[i] = mm(xu[...], w1b[:, i * fc:i * fc + fc])

    def gelu(i):
        cols = slice(i * fc, i * fc + fc)
        for r in range(0, tok, STRIP):
            rs = slice(r, r + STRIP)
            x = slope[i, rs, :]
            x2 = x * x
            t = jnp.tanh(x * (GELU_C + (GELU_C * GELU_A) * x2))
            t1 = 1.0 + t
            g = (0.5 * x) * t1
            act[rs, cols] = g.astype(BF)
            slope[i, rs, :] = 0.5 * t1 + (g * (1.0 - t)) * (GELU_C + (3.0 * GELU_C * GELU_A) * x2)

    waits = {1: (1, 2), 3: tuple(range(3, n_ch))}
    for i in range(n_ch):
        for w in waits.get(i, ()):
            load_w1[w].wait()
        pre(i)
        if i:
            gelu(i - 1)
    for w in load_w2:
        w.wait()
    load_l.wait()
    gelu(n_ch - 1)
    zc = d_model // 2
    for n in range(2):
        cs = slice(n * zc, n * zc + zc)
        zz = mm(act[...], w2[:, cs])
        for r in range(0, tok, STRIP):
            rs = slice(r, r + STRIP)
            z[rs, cs] = (xu[rs, cs].astype(F32) + zz[rs]).astype(BF)

    logits = mm(head_t[...], z[...], NT)
    rows = lax.broadcasted_iota(jnp.int32, (32, tok), 0)
    for t in range(n_task):
        lg = jnp.where(rows < n_cls, logits[32 * t:32 * t + 32], -jnp.inf)
        ex = jnp.exp(lg - jnp.max(lg, axis=0, keepdims=True))
        prob = ex / jnp.sum(ex, axis=0, keepdims=True)
        err = (prob - (rows == lab_v[t:t + 1, :]).astype(F32)).astype(BF)
        dz[tok * t:tok * t + tok, :] = mm(err, head_t[32 * t:32 * t + 32, :], TN).astype(BF)

    pl.semaphore_wait(barrier, n_dev - 1)

    def chunk_of(kk):
        return xor(chip, kk)

    def b_copy(t, kk, half):
        k = 2 * kk + (core + half) % 2
        return pltpu.make_async_remote_copy(
            src_ref=send_b.at[t, kk, half], dst_ref=recv_b.at[t, k - 1], send_sem=sb_sem.at[t], recv_sem=rb_sem.at[t],
            device_id=(2 * chunk_of(kk) + half,), device_id_type=MESH)

    def a_copy(t, k):
        dst = xor(me, k)
        return pltpu.make_async_remote_copy(
            src_ref=send_a.at[t, dst], dst_ref=recv_a.at[t, k - 1], send_sem=sa_sem.at[t], recv_sem=ra_sem.at[t],
            device_id=(dst,), device_id_type=MESH)

    def m_copy(k):
        return pltpu.make_async_remote_copy(
            src_ref=send_m, dst_ref=recv_m.at[k - 1], send_sem=sm_sem.at[0], recv_sem=rm_sem.at[0],
            device_id=(xor(me, k),), device_id_type=MESH)

    order = [15, 14, 13, 11, 10, 7, 6, 12, 9, 5, 3, 8, 4, 2, 1]
    lane8 = lax.broadcasted_iota(jnp.int32, (8, 128), 1)

    def wait_all(ref, sem):
        pltpu.make_async_copy(ref, ref, sem).wait()

    def d_pre(j, dp_ref):
        t, c = j // n_ch, chunk_of(n_ch - 1 - j % n_ch)
        dh = mm(dz[pl.ds(pl.multiple_of(t * tok, tok), tok), :], w2[pl.ds(pl.multiple_of(c * fc, fc), fc), :], NT)
        for r in range(0, tok, STRIP):
            rs = slice(r, r + STRIP)
            dp_ref[rs, :] = (dh[rs] * slope[c, rs, :]).astype(BF)

    def grads(j, dp_ref):
        t, kk = j // n_ch, n_ch - 1 - j % n_ch
        c = chunk_of(kk)
        bm = w1b[pl.ds(d_model, rank), pl.ds(pl.multiple_of(c * fc, fc), fc)]
        du_t[t] += mm(bm, dp_ref[...], NT)
        gb = mm(u_t[...], dp_ref[...])
        for half in range(2):
            send_b[t, kk, half] = gb[:, col * half:col * half + col]
        return t, kk

    def low_grad(t):
        ga = mm(du_t[t].astype(BF), xu[:, :d_model])
        for j in range(n_ch):
            top, low = ga[0:8, 128 * j:128 * j + 128], ga[8:16, 128 * j:128 * j + 128]
            send_a[t, 2 * j] = jnp.where(lane8 < 64, top, pltpu.roll(low, 64, 1))
            send_a[t, 2 * j + 1] = jnp.where(lane8 < 64, pltpu.roll(top, 64, 1), low)
        for k in order:
            a_copy(t, k).start()

    n_unit = n_task * n_ch
    d_pre(0, dp0)

    def bwd(i, _):
        d_pre(2 * i + 1, dp1)
        t, kk = grads(2 * i, dp0)
        d_pre(2 * i + 2, dp0)
        b_copy(t, kk, 0).start()
        b_copy(t, kk, 1).start()
        t, kk = grads(2 * i + 1, dp1)

        @pl.when(i != n_ch // 2 - 1)
        def _():
            b_copy(t, kk, 0).start()
            b_copy(t, kk, 1).start()

        @pl.when(i == n_ch // 2 - 1)
        def _():
            b_copy(0, 0, 1 - core).start()
            low_grad(0)

        return 0

    lax.fori_loop(0, n_unit // 2 - 1, bwd, 0)
    d_pre(n_unit - 1, dp1)
    t, kk = grads(n_unit - 2, dp0)
    b_copy(t, kk, 0).start()
    b_copy(t, kk, 1).start()
    grads(n_unit - 1, dp1)
    low_grad(1)
    b_copy(1, 0, 1 - core).start()

    inv = 1.0 / total

    def sum_up(own, recv, sem):
        wait_all(recv, sem)
        s = own
        for k in range(n_dev - 1):
            s = s + recv[k]
        return s * inv

    b_sum = [sum_up(send_b[t, 0, core], recv_b.at[t], rb_sem.at[t]) for t in range(n_task)]
    a_sum = [sum_up(send_a[t, me], recv_a.at[t], ra_sem.at[t]) for t in range(n_task)]

    def fold(part_b, part_a):
        return jnp.sum(part_b[:8, :128] + part_b[:8, 128:] + part_b[8:, :128] + part_b[8:, 128:] + part_a, axis=0, keepdims=True)

    b0, b1 = b_sum
    a0, a1 = a_sum
    s0 = fold(b0 * b0, a0 * a0)
    s1 = fold(b1 * b1, a1 * a1)
    mix = fold(b0 * b1, a0 * a1)
    send_m[0:1, :] = s0 - s1
    send_m[1:2, :] = s0 + s1
    send_m[2:3, :] = mix
    send_m[3:4, :] = jnp.zeros_like(mix)
    for k in order:
        m_copy(k).start()
    sum_m = send_m[...]
    wait_all(recv_m, rm_sem.at[0])
    for k in range(n_dev - 1):
        sum_m = sum_m + recv_m[k]
    gram = jnp.broadcast_to(jnp.sum(sum_m, axis=1, keepdims=True), sum_m.shape)
    m_diff, m_both, m_mix = gram[0:1], gram[1:2], gram[2:3]
    scale = 0.5 / m_both
    c0 = m_diff * scale
    c1 = (m_both - 2.0 * m_mix) * scale
    e = jnp.zeros_like(c0)
    for _ in range(EG_STEPS):
        e = e - (c0 + c1 * jnp.tanh(e))
    al0 = 1.0 / (1.0 + jnp.exp(-2.0 * e))
    al1 = 1.0 / (1.0 + jnp.exp(2.0 * e))
    gb_ref[...] = al0[:, 0:1] * b0 + al1[:, 0:1] * b1
    comb = al0 * a0 + al1 * a1
    ga_ref[0:8, :] = comb[:, :64]
    ga_ref[8:16, :] = pltpu.roll(comb, 64, 1)[:, :64]
    alpha_ref[...] = jnp.where(lane8[0:1, :] == 0, al0, al1)[:, 0:2]
    for t in range(n_task):
        wait_all(recv_b.at[t], sb_sem.at[t])
        wait_all(recv_a.at[t], sa_sem.at[t])
    wait_all(recv_m, sm_sem.at[0])


def finish(alpha_in, ga_in, gb_in, alpha_ref, ga_ref, gb_ref):
    alpha_ref[...] = alpha_in[...]
    ga_ref[...] = ga_in[...]
    gb_ref[...] = gb_in[...]


def solution(mesh):
    n_dev = mesh.shape["data"]

    def device_step(tokens, labels, w_one, w_two, adapter_a, adapter_b, task_heads):
        tok, d_model = tokens.shape
        d_ff = w_one.shape[1]
        rank = adapter_a.shape[1]
        n_tasks, _, n_cls = task_heads.shape
        col = d_ff // n_dev
        fc = 2 * col
        dma = pltpu.SemaphoreType.DMA
        outs = pl.pallas_call(
            functools.partial(kernel, (n_dev, tok * n_dev)),
            out_shape=(
                jax.ShapeDtypeStruct((1, n_tasks), F32),
                jax.ShapeDtypeStruct((rank, d_model // n_dev), F32),
                jax.ShapeDtypeStruct((rank, col), F32),
            ),
            in_specs=[pl.BlockSpec(memory_space=pl.ANY)] * 7,
            out_specs=[pl.BlockSpec(memory_space=pltpu.VMEM)] * 3,
            scratch_shapes=[
                pltpu.VMEM((tok, d_model + 128), BF),
                pltpu.VMEM((d_model + 128, d_ff), BF),
                pltpu.VMEM((d_ff, d_model), BF),
                pltpu.VMEM((rank, d_model), BF),
                pltpu.VMEM((n_cls, n_tasks, d_model), BF),
                pltpu.VMEM((n_tasks, tok), jnp.int32),
                pltpu.VMEM((n_tasks * 32, d_model), BF),
                pltpu.VMEM((rank, tok), BF),
                pltpu.VMEM((tok, d_ff), BF),
                pltpu.VMEM((n_dev // 2, tok, fc), F32),
                pltpu.VMEM((tok, d_model), BF),
                pltpu.VMEM((n_tasks * tok, d_model), BF),
                pltpu.VMEM((tok, fc), BF),
                pltpu.VMEM((tok, fc), BF),
                pltpu.VMEM((n_tasks, rank, tok), F32),
                pltpu.VMEM((n_tasks, n_dev // 2, 2, rank, col), F32),
                pltpu.VMEM((n_tasks, n_dev - 1, rank, col), F32),
                pltpu.VMEM((n_tasks, n_dev, 8, 128), F32),
                pltpu.VMEM((n_tasks, n_dev - 1, 8, 128), F32),
                pltpu.VMEM((4, 128), F32),
                pltpu.VMEM((n_dev - 1, 4, 128), F32),
                dma((n_dev // 2 + 9,)),
                dma((n_tasks,)), dma((n_tasks,)), dma((n_tasks,)), dma((n_tasks,)), dma((1,)), dma((1,)),
            ],
            compiler_params=pltpu.CompilerParams(collective_id=0, has_side_effects=True, vmem_limit_bytes=60 * 1024 * 1024),
            name="step",
        )(tokens, labels, w_one, w_two, adapter_a.T, adapter_b, task_heads.transpose(2, 0, 1))
        alpha, ga, gb = pl.pallas_call(
            finish,
            out_shape=[jax.ShapeDtypeStruct(o.shape, o.dtype) for o in outs],
            in_specs=[pl.BlockSpec(memory_space=pltpu.VMEM)] * 3,
            out_specs=[pl.BlockSpec(memory_space=pltpu.VMEM)] * 3,
            name="finish",
        )(*outs)
        return alpha.reshape(n_tasks), ga.T, gb

    return jax.shard_map(device_step, mesh=mesh, in_specs=(P("data", None), P(None, "data"), P(), P(), P(), P(), P()), out_specs=(P(), P("data", None), P(None, "data")), check_vma=False)
```

time: 46.9 us -> 45.7 us (0.974)
  Pallas kernels: 46.1 us -> 44.9 us
    pallas_call x1, Pallas kernels: 44.8 us -> 43.5 us  [device_step(): pl.pallas_call(functools.partial(kernel, (n_dev, tok * n_dev)), out_shape...]
where the time goes in v3:
time: 45.7 us; the launch traced here: 45.5 us
  Pallas kernels  44.9 us (98%)
  between operations  0.64 us (1%)
    pallas_call x1, Pallas kernels, device_step(): pl.pallas_call(functools.partial(kernel, (n_dev, tok * n_dev)), out_shape...  43.5 us
    pallas_call x1, Pallas kernels, device_step(): pl.pallas_call(finish, out_shape=[jax.ShapeDtypeStruct(o.shape, o.dtype)...  1.36 us

profile of v3, /device:TPU:0, one launch (start us, length us, event | category | flops | bytes accessed | tf_op | source)
XLA Modules:
  0.0 45.5 jit_solution(8147305531249102787)
XLA Ops:
  0.6 43.5 %step.1 = (f32[1,2]{1,0:T(1,128)}, f32[16,64]{1,0:T(8,128)}, f32[16,256]{1,0:T(8,128)}) custom-call(bf16[512,1024]{1,0:T(8,128)(2,1)} %x_hbm.1, s32[2,512]{1,0:T(2,128)} %lab_hbm.1, bf16[1024,4096]{1,0:T(8,128)(2,1)} %w1_hbm.1, bf16[4096,1024]{1,0:T(8,128)(2,1)} %w2_hbm.1, bf16[16,1024]{1,0:T(8,128)(2,1)} %bitcast.5, bf16[16,4096]{1,0:T(8,128)(2,1)} %b_hbm.1, ...), custom_call_target="tpu_custom_call" | custom-call | tf_op jit(solution)/shard_map/step/pallas_call | solution.py:276
  44.2 1.4 %finish.1 = (f32[1,2]{1,0:T(1,128)}, f32[16,64]{1,0:T(8,128)}, f32[16,256]{1,0:T(8,128)}) custom-call(f32[1,2]{1,0:T(1,128)} %get-tuple-element.9.alpha_in, f32[16,64]{1,0:T(8,128)} %get-tuple-element.10.ga_in, f32[16,256]{1,0:T(8,128)} %get-tuple-element.11.gb_in), custom_call_target="tpu_custom_call" | custom-call | tf_op jit(solution)/shard_map/finish/pallas_call | solution.py:313

commit v4 on v3

--- a/solution.py
+++ b/solution.py
@@ -64,7 +64,6 @@
     xu[:, d_model:] = jnp.zeros((tok, pad), BF)
     w1b[d_model + rank:, :] = jnp.zeros((pad - rank, d_ff), BF)
     head_t[...] = jnp.zeros_like(head_t)
-    du_t[...] = jnp.zeros_like(du_t)
     load_h.wait()
     for t in range(n_task):
         head_t[32 * t:32 * t + n_cls, :] = head_v[:, t, :]
@@ -91,33 +90,61 @@
             act[rs, cols] = g.astype(BF)
             slope[i, rs, :] = 0.5 * t1 + (g * (1.0 - t)) * (GELU_C + (3.0 * GELU_C * GELU_A) * x2)
 
-    waits = {1: (1, 2), 3: tuple(range(3, n_ch))}
-    for i in range(n_ch):
-        for w in waits.get(i, ()):
-            load_w1[w].wait()
-        pre(i)
-        if i:
-            gelu(i - 1)
+    def stage(first, last):
+        @pl.when(me >= 0)
+        def _():
+            for i in range(first, last):
+                pre(i)
+                if i:
+                    gelu(i - 1)
+
+    stage(0, 1)
+    for w in load_w1[1:3]:
+        w.wait()
+    stage(1, 3)
+    for w in load_w1[3:]:
+        w.wait()
+    stage(3, n_ch)
     for w in load_w2:
         w.wait()
     load_l.wait()
-    gelu(n_ch - 1)
+    hl = tok // 2
     zc = d_model // 2
-    for n in range(2):
+
+    def out_block(h, n):
         cs = slice(n * zc, n * zc + zc)
-        zz = mm(act[...], w2[:, cs])
-        for r in range(0, tok, STRIP):
-            rs = slice(r, r + STRIP)
-            z[rs, cs] = (xu[rs, cs].astype(F32) + zz[rs]).astype(BF)
-
-    logits = mm(head_t[...], z[...], NT)
-    rows = lax.broadcasted_iota(jnp.int32, (32, tok), 0)
-    for t in range(n_task):
-        lg = jnp.where(rows < n_cls, logits[32 * t:32 * t + 32], -jnp.inf)
-        ex = jnp.exp(lg - jnp.max(lg, axis=0, keepdims=True))
-        prob = ex / jnp.sum(ex, axis=0, keepdims=True)
-        err = (prob - (rows == lab_v[t:t + 1, :]).astype(F32)).astype(BF)
-        dz[tok * t:tok * t + tok, :] = mm(err, head_t[32 * t:32 * t + 32, :], TN).astype(BF)
+        zz = mm(act[h * hl:h * hl + hl, :], w2[:, cs])
+        for r in range(0, hl, STRIP):
+            rs = slice(h * hl + r, h * hl + r + STRIP)
+            z[rs, cs] = (xu[rs, cs].astype(F32) + zz[r:r + STRIP]).astype(BF)
+
+    def errors(h):
+        hs = slice(h * hl, h * hl + hl)
+        logits = mm(head_t[...], z[hs, :], NT)
+        rows = lax.broadcasted_iota(jnp.int32, (32, hl), 0)
+        out = []
+        for t in range(n_task):
+            lg = jnp.where(rows < n_cls, logits[32 * t:32 * t + 32], -jnp.inf)
+            ex = jnp.exp(lg - jnp.max(lg, axis=0, keepdims=True))
+            prob = ex / jnp.sum(ex, axis=0, keepdims=True)
+            out.append((prob - (rows == lab_v[t:t + 1, hs]).astype(F32)).astype(BF))
+        return out
+
+    def d_trunk(h, errs):
+        for t in range(n_task):
+            dz[tok * t + h * hl:tok * t + h * hl + hl, :] = mm(errs[t], head_t[32 * t:32 * t + 32, :], TN).astype(BF)
+
+    @pl.when(me >= 0)
+    def _():
+        gelu(n_ch - 1)
+        out_block(0, 0)
+        out_block(0, 1)
+        out_block(1, 0)
+        errs0 = errors(0)
+        out_block(1, 1)
+        errs1 = errors(1)
+        d_trunk(0, errs0)
+        d_trunk(1, errs1)
 
     pl.semaphore_wait(barrier, n_dev - 1)
 
@@ -147,25 +174,24 @@
     def wait_all(ref, sem):
         pltpu.make_async_copy(ref, ref, sem).wait()
 
-    def d_pre(j, dp_ref):
-        t, c = j // n_ch, chunk_of(n_ch - 1 - j % n_ch)
+    def d_pre(t, kk, dp_ref):
+        c = chunk_of(kk)
         dh = mm(dz[pl.ds(pl.multiple_of(t * tok, tok), tok), :], w2[pl.ds(pl.multiple_of(c * fc, fc), fc), :], NT)
         for r in range(0, tok, STRIP):
             rs = slice(r, r + STRIP)
             dp_ref[rs, :] = (dh[rs] * slope[c, rs, :]).astype(BF)
 
-    def grads(j, dp_ref):
-        t, kk = j // n_ch, n_ch - 1 - j % n_ch
+    def grads(t, kk, dp_ref):
         c = chunk_of(kk)
         bm = w1b[pl.ds(d_model, rank), pl.ds(pl.multiple_of(c * fc, fc), fc)]
-        du_t[t] += mm(bm, dp_ref[...], NT)
+        part = mm(bm, dp_ref[...], NT)
+        du_t[...] = part if kk == n_ch - 1 else du_t[...] + part
         gb = mm(u_t[...], dp_ref[...])
         for half in range(2):
             send_b[t, kk, half] = gb[:, col * half:col * half + col]
-        return t, kk
 
     def low_grad(t):
-        ga = mm(du_t[t].astype(BF), xu[:, :d_model])
+        ga = mm(du_t[...].astype(BF), xu[:, :d_model])
         for j in range(n_ch):
             top, low = ga[0:8, 128 * j:128 * j + 128], ga[8:16, 128 * j:128 * j + 128]
             send_a[t, 2 * j] = jnp.where(lane8 < 64, top, pltpu.roll(low, 64, 1))
@@ -173,37 +199,24 @@
         for k in order:
             a_copy(t, k).start()
 
-    n_unit = n_task * n_ch
-    d_pre(0, dp0)
-
-    def bwd(i, _):
-        d_pre(2 * i + 1, dp1)
-        t, kk = grads(2 * i, dp0)
-        d_pre(2 * i + 2, dp0)
-        b_copy(t, kk, 0).start()
-        b_copy(t, kk, 1).start()
-        t, kk = grads(2 * i + 1, dp1)
-
-        @pl.when(i != n_ch // 2 - 1)
-        def _():
-            b_copy(t, kk, 0).start()
-            b_copy(t, kk, 1).start()
-
-        @pl.when(i == n_ch // 2 - 1)
-        def _():
-            b_copy(0, 0, 1 - core).start()
-            low_grad(0)
-
+    def task(t, _):
+        dps = (dp0, dp1)
+        d_pre(t, n_ch - 1, dps[1])
+        for kk in reversed(range(n_ch)):
+            if kk:
+                d_pre(t, kk - 1, dps[(kk - 1) % 2])
+            grads(t, kk, dps[kk % 2])
+            if kk and kk % 2 == 0:
+                for k2 in (kk + 1, kk):
+                    b_copy(t, k2, 0).start()
+                    b_copy(t, k2, 1).start()
+        low_grad(t)
+        b_copy(t, 1, 0).start()
+        b_copy(t, 1, 1).start()
+        b_copy(t, 0, 1 - core).start()
         return 0
 
-    lax.fori_loop(0, n_unit // 2 - 1, bwd, 0)
-    d_pre(n_unit - 1, dp1)
-    t, kk = grads(n_unit - 2, dp0)
-    b_copy(t, kk, 0).start()
-    b_copy(t, kk, 1).start()
-    grads(n_unit - 1, dp1)
-    low_grad(1)
-    b_copy(1, 0, 1 - core).start()
+    lax.fori_loop(0, n_task, task, 0)
 
     inv = 1.0 / total
 
@@ -297,7 +310,7 @@
                 pltpu.VMEM((n_tasks * tok, d_model), BF),
                 pltpu.VMEM((tok, fc), BF),
                 pltpu.VMEM((tok, fc), BF),
-                pltpu.VMEM((n_tasks, rank, tok), F32),
+                pltpu.VMEM((rank, tok), F32),
                 pltpu.VMEM((n_tasks, n_dev // 2, 2, rank, col), F32),
                 pltpu.VMEM((n_tasks, n_dev - 1, rank, col), F32),
                 pltpu.VMEM((n_tasks, n_dev, 8, 128), F32),

time: 45.7 us -> 43.8 us (0.958)
  Pallas kernels: 44.9 us -> 42.9 us
    pallas_call x1, Pallas kernels: 43.5 us -> 41.6 us  [device_step(): pl.pallas_call(functools.partial(kernel, (n_dev, tok * n_dev)), out_shape...]
where the time goes in v4:
time: 43.8 us; the launch traced here: 43.6 us
  Pallas kernels  42.9 us (98%)
  between operations  0.64 us (1%)
    pallas_call x1, Pallas kernels, device_step(): pl.pallas_call(functools.partial(kernel, (n_dev, tok * n_dev)), out_shape...  41.6 us
    pallas_call x1, Pallas kernels, device_step(): pl.pallas_call(finish, out_shape=[jax.ShapeDtypeStruct(o.shape, o.dtype)...  1.36 us

profile of v4, /device:TPU:0, one launch (start us, length us, event | category | flops | bytes accessed | tf_op | source)
XLA Modules:
  0.0 43.6 jit_solution(16960999825039601549)
XLA Ops:
  0.6 41.6 %step.1 = (f32[1,2]{1,0:T(1,128)}, f32[16,64]{1,0:T(8,128)}, f32[16,256]{1,0:T(8,128)}) custom-call(bf16[512,1024]{1,0:T(8,128)(2,1)} %x_hbm.1, s32[2,512]{1,0:T(2,128)} %lab_hbm.1, bf16[1024,4096]{1,0:T(8,128)(2,1)} %w1_hbm.1, bf16[4096,1024]{1,0:T(8,128)(2,1)} %w2_hbm.1, bf16[16,1024]{1,0:T(8,128)(2,1)} %bitcast.5, bf16[16,4096]{1,0:T(8,128)(2,1)} %b_hbm.1, ...), custom_call_target="tpu_custom_call" | custom-call | tf_op jit(solution)/shard_map/step/pallas_call | solution.py:289
  42.2 1.4 %finish.1 = (f32[1,2]{1,0:T(1,128)}, f32[16,64]{1,0:T(8,128)}, f32[16,256]{1,0:T(8,128)}) custom-call(f32[1,2]{1,0:T(1,128)} %get-tuple-element.9.alpha_in, f32[16,64]{1,0:T(8,128)} %get-tuple-element.10.ga_in, f32[16,256]{1,0:T(8,128)} %get-tuple-element.11.gb_in), custom_call_target="tpu_custom_call" | custom-call | tf_op jit(solution)/shard_map/finish/pallas_call | solution.py:326

commit v5 on v4

--- a/solution.py
+++ b/solution.py
@@ -70,7 +70,6 @@
     load_a.wait()
     load_b.wait()
     load_x.wait()
-    load_w1[0].wait()
     low = mm(xu[:, :d_model], a_v[...], NT)
     xu[:, d_model:d_model + rank] = low.astype(BF)
     u_t[...] = low.T.astype(BF)
@@ -98,6 +97,7 @@
                 if i:
                     gelu(i - 1)
 
+    load_w1[0].wait()
     stage(0, 1)
     for w in load_w1[1:3]:
         w.wait()
@@ -177,9 +177,7 @@
     def d_pre(t, kk, dp_ref):
         c = chunk_of(kk)
         dh = mm(dz[pl.ds(pl.multiple_of(t * tok, tok), tok), :], w2[pl.ds(pl.multiple_of(c * fc, fc), fc), :], NT)
-        for r in range(0, tok, STRIP):
-            rs = slice(r, r + STRIP)
-            dp_ref[rs, :] = (dh[rs] * slope[c, rs, :]).astype(BF)
+        dp_ref[...] = (dh * slope[c]).astype(BF)
 
     def grads(t, kk, dp_ref):
         c = chunk_of(kk)
@@ -199,6 +197,8 @@
         for k in order:
             a_copy(t, k).start()
 
+    groups = {4: (7, 6, 5, 4), 2: (3, 2)}
+
     def task(t, _):
         dps = (dp0, dp1)
         d_pre(t, n_ch - 1, dps[1])
@@ -206,10 +206,9 @@
             if kk:
                 d_pre(t, kk - 1, dps[(kk - 1) % 2])
             grads(t, kk, dps[kk % 2])
-            if kk and kk % 2 == 0:
-                for k2 in (kk + 1, kk):
-                    b_copy(t, k2, 0).start()
-                    b_copy(t, k2, 1).start()
+            for k2 in groups.get(kk, ()):
+                b_copy(t, k2, 0).start()
+                b_copy(t, k2, 1).start()
         low_grad(t)
         b_copy(t, 1, 0).start()
         b_copy(t, 1, 1).start()
@@ -255,7 +254,7 @@
     c1 = (m_both - 2.0 * m_mix) * scale
     e = jnp.zeros_like(c0)
     for _ in range(EG_STEPS):
-        e = e - (c0 + c1 * jnp.tanh(e))
+        e = (e - c0) - c1 * jnp.tanh(e)
     al0 = 1.0 / (1.0 + jnp.exp(-2.0 * e))
     al1 = 1.0 / (1.0 + jnp.exp(2.0 * e))
     gb_ref[...] = al0[:, 0:1] * b0 + al1[:, 0:1] * b1
@@ -289,9 +288,9 @@
         outs = pl.pallas_call(
             functools.partial(kernel, (n_dev, tok * n_dev)),
             out_shape=(
-                jax.ShapeDtypeStruct((1, n_tasks), F32),
-                jax.ShapeDtypeStruct((rank, d_model // n_dev), F32),
-                jax.ShapeDtypeStruct((rank, col), F32),
+                pltpu.VMEM((1, n_tasks), F32),
+                pltpu.VMEM((rank, d_model // n_dev), F32),
+                pltpu.VMEM((rank, col), F32),
             ),
             in_specs=[pl.BlockSpec(memory_space=pl.ANY)] * 7,
             out_specs=[pl.BlockSpec(memory_space=pltpu.VMEM)] * 3,
@@ -329,7 +328,7 @@
             in_specs=[pl.BlockSpec(memory_space=pltpu.VMEM)] * 3,
             out_specs=[pl.BlockSpec(memory_space=pltpu.VMEM)] * 3,
             name="finish",
-        )(*outs)
+        )(*[pltpu.with_memory_space_constraint(o, pltpu.VMEM) for o in outs])
         return alpha.reshape(n_tasks), ga.T, gb
 
     return jax.shard_map(device_step, mesh=mesh, in_specs=(P("data", None), P(None, "data"), P(), P(), P(), P(), P()), out_specs=(P(), P("data", None), P(None, "data")), check_vma=False)

time: 43.8 us -> 41.7 us (0.952)
  Pallas kernels: 42.9 us -> 41 us
    pallas_call x1, Pallas kernels: 41.6 us -> 40.3 us  [device_step(): pl.pallas_call(functools.partial(kernel, (n_dev, tok * n_dev)), out_shape...]
    pallas_call x1, Pallas kernels: 1.36 us -> 0.62 us  [device_step(): pl.pallas_call(finish, out_shape=[jax.ShapeDtypeStruct(o.shape, o.dtype)...]
where the time goes in v5:
time: 41.7 us; the launch traced here: 41.6 us
  Pallas kernels  41 us (98%)
  between operations  0.64 us (2%)
    pallas_call x1, Pallas kernels, device_step(): pl.pallas_call(functools.partial(kernel, (n_dev, tok * n_dev)), out_shape...  40.3 us

profile of v5, /device:TPU:0, one launch (start us, length us, event | category | flops | bytes accessed | tf_op | source)
XLA Modules:
  0.0 41.6 jit_solution(9382981936375559982)
XLA Ops:
  0.6 40.3 %step.1 = (f32[1,2]{1,0:T(1,128)S(1)}, f32[16,64]{1,0:T(8,128)S(1)}, f32[16,256]{1,0:T(8,128)S(1)}) custom-call(bf16[512,1024]{1,0:T(8,128)(2,1)} %x_hbm.1, s32[2,512]{1,0:T(2,128)} %lab_hbm.1, bf16[1024,4096]{1,0:T(8,128)(2,1)} %w1_hbm.1, bf16[4096,1024]{1,0:T(8,128)(2,1)} %w2_hbm.1, bf16[16,1024]{1,0:T(8,128)(2,1)} %bitcast.5, bf16[16,4096]{1,0:T(8,128)(2,1)} %b_hbm.1, ...), custom_call_target="tpu_custom_call" | custom-call | tf_op jit(solution)/shard_map/step/pallas_call | solution.py:288
  41.0 0.6 %finish.1 = (f32[1,2]{1,0:T(1,128)}, f32[16,64]{1,0:T(8,128)}, f32[16,256]{1,0:T(8,128)}) custom-call(f32[1,2]{1,0:T(1,128)S(1)} %get-tuple-element.9.alpha_in, f32[16,64]{1,0:T(8,128)S(1)} %get-tuple-element.10.ga_in, f32[16,256]{1,0:T(8,128)S(1)} %get-tuple-element.11.gb_in), custom_call_target="tpu_custom_call" | custom-call | tf_op jit(solution)/shard_map/finish/pallas_call | solution.py:325

commit v6 on v5

--- a/solution.py
+++ b/solution.py
@@ -27,7 +27,7 @@
     return lax.dot_general(a, b, dims, preferred_element_type=F32)
 
 
-def kernel(cfg, x_hbm, lab_hbm, w1_hbm, w2_hbm, a_hbm, b_hbm, head_hbm, alpha_ref, ga_ref, gb_ref, xu, w1b, w2, a_v, head_v, lab_v, head_t, u_t, act, slope, z, dz, dp0, dp1, du_t, send_b, recv_b, send_a, recv_a, send_m, recv_m, load_sem, sb_sem, rb_sem, sa_sem, ra_sem, sm_sem, rm_sem):
+def kernel(cfg, x_hbm, lab_hbm, w1_hbm, w2_hbm, a_hbm, b_hbm, head_hbm, alpha_ref, ga_ref, gb_ref, xu, w1b, w2, a_v, head_v, lab_v, head_t, u_t, act, slope, z, dz, dp0, dp1, dpt0, dpt1, du_t, send_b, recv_b, send_a, recv_a, send_m, recv_m, load_sem, sb_sem, rb_sem, sa_sem, ra_sem, sm_sem, rm_sem):
     n_dev, total = cfg
     tok, d_model = x_hbm.shape
     d_ff = w1_hbm.shape[1]
@@ -174,22 +174,24 @@
     def wait_all(ref, sem):
         pltpu.make_async_copy(ref, ref, sem).wait()
 
-    def d_pre(t, kk, dp_ref):
+    def d_pre(t, kk, dp_ref, dpt_ref):
         c = chunk_of(kk)
-        dh = mm(dz[pl.ds(pl.multiple_of(t * tok, tok), tok), :], w2[pl.ds(pl.multiple_of(c * fc, fc), fc), :], NT)
-        dp_ref[...] = (dh * slope[c]).astype(BF)
-
-    def grads(t, kk, dp_ref):
+        dh = mm(dz[tok * t:tok * t + tok, :], w2[pl.ds(pl.multiple_of(c * fc, fc), fc), :], NT)
+        dp = (dh * slope[c]).astype(BF)
+        dp_ref[...] = dp
+        dpt_ref[...] = dp.T
+
+    def grads(t, kk, dp_ref, dpt_ref):
         c = chunk_of(kk)
         bm = w1b[pl.ds(d_model, rank), pl.ds(pl.multiple_of(c * fc, fc), fc)]
-        part = mm(bm, dp_ref[...], NT)
-        du_t[...] = part if kk == n_ch - 1 else du_t[...] + part
+        part = mm(bm, dpt_ref[...])
+        du_t[t] = part if kk == n_ch - 1 else du_t[t] + part
         gb = mm(u_t[...], dp_ref[...])
         for half in range(2):
             send_b[t, kk, half] = gb[:, col * half:col * half + col]
 
     def low_grad(t):
-        ga = mm(du_t[...].astype(BF), xu[:, :d_model])
+        ga = mm(du_t[t].astype(BF), xu[:, :d_model])
         for j in range(n_ch):
             top, low = ga[0:8, 128 * j:128 * j + 128], ga[8:16, 128 * j:128 * j + 128]
             send_a[t, 2 * j] = jnp.where(lane8 < 64, top, pltpu.roll(low, 64, 1))
@@ -197,25 +199,29 @@
         for k in order:
             a_copy(t, k).start()
 
-    groups = {4: (7, 6, 5, 4), 2: (3, 2)}
-
-    def task(t, _):
-        dps = (dp0, dp1)
-        d_pre(t, n_ch - 1, dps[1])
-        for kk in reversed(range(n_ch)):
+    def send_group(t, group):
+        for kk in group:
             if kk:
-                d_pre(t, kk - 1, dps[(kk - 1) % 2])
-            grads(t, kk, dps[kk % 2])
-            for k2 in groups.get(kk, ()):
-                b_copy(t, k2, 0).start()
-                b_copy(t, k2, 1).start()
-        low_grad(t)
-        b_copy(t, 1, 0).start()
-        b_copy(t, 1, 1).start()
-        b_copy(t, 0, 1 - core).start()
-        return 0
-
-    lax.fori_loop(0, n_task, task, 0)
+                b_copy(t, kk, 0).start()
+                b_copy(t, kk, 1).start()
+            else:
+                b_copy(t, 0, 1 - core).start()
+
+    units = [(t, kk) for t in range(n_task) for kk in reversed(range(n_ch))]
+    dps = (dp0, dp1)
+    dpts = (dpt0, dpt1)
+    d_pre(*units[0], dps[0], dpts[0])
+    for j, (t, kk) in enumerate(units):
+        if j + 1 < len(units):
+            d_pre(*units[j + 1], dps[(j + 1) % 2], dpts[(j + 1) % 2])
+        grads(t, kk, dps[j % 2], dpts[j % 2])
+        if kk == 4:
+            send_group(t, (7, 6, 5, 4))
+        if kk == 2 and t == n_task - 1:
+            send_group(t, (3, 2))
+        if kk == 0:
+            low_grad(t)
+            send_group(t, (1, 0) if t == n_task - 1 else (3, 2, 1, 0))
 
     inv = 1.0 / total
 
@@ -309,7 +315,9 @@
                 pltpu.VMEM((n_tasks * tok, d_model), BF),
                 pltpu.VMEM((tok, fc), BF),
                 pltpu.VMEM((tok, fc), BF),
-                pltpu.VMEM((rank, tok), F32),
+                pltpu.VMEM((fc, tok), BF),
+                pltpu.VMEM((fc, tok), BF),
+                pltpu.VMEM((n_tasks, rank, tok), F32),
                 pltpu.VMEM((n_tasks, n_dev // 2, 2, rank, col), F32),
                 pltpu.VMEM((n_tasks, n_dev - 1, rank, col), F32),
                 pltpu.VMEM((n_tasks, n_dev, 8, 128), F32),

time: 41.7 us -> 41.1 us (0.986)
  Pallas kernels: 41 us -> 40.3 us
    pallas_call x1, Pallas kernels: 40.3 us -> 39.7 us  [device_step(): pl.pallas_call(functools.partial(kernel, (n_dev, tok * n_dev)), out_shape...]
where the time goes in v6:
time: 41.1 us; the launch traced here: 41 us
  Pallas kernels  40.3 us (98%)
  between operations  0.64 us (2%)
    pallas_call x1, Pallas kernels, device_step(): pl.pallas_call(functools.partial(kernel, (n_dev, tok * n_dev)), out_shape...  39.7 us

profile of v6, /device:TPU:0, one launch (start us, length us, event | category | flops | bytes accessed | tf_op | source)
XLA Modules:
  0.0 41.0 jit_solution(12714065691688467015)
XLA Ops:
  0.6 39.7 %step.1 = (f32[1,2]{1,0:T(1,128)S(1)}, f32[16,64]{1,0:T(8,128)S(1)}, f32[16,256]{1,0:T(8,128)S(1)}) custom-call(bf16[512,1024]{1,0:T(8,128)(2,1)} %x_hbm.1, s32[2,512]{1,0:T(2,128)} %lab_hbm.1, bf16[1024,4096]{1,0:T(8,128)(2,1)} %w1_hbm.1, bf16[4096,1024]{1,0:T(8,128)(2,1)} %w2_hbm.1, bf16[16,1024]{1,0:T(8,128)(2,1)} %bitcast.5, bf16[16,4096]{1,0:T(8,128)(2,1)} %b_hbm.1, ...), custom_call_target="tpu_custom_call" | custom-call | tf_op jit(solution)/shard_map/step/pallas_call | solution.py:294
  40.3 0.6 %finish.1 = (f32[1,2]{1,0:T(1,128)}, f32[16,64]{1,0:T(8,128)}, f32[16,256]{1,0:T(8,128)}) custom-call(f32[1,2]{1,0:T(1,128)S(1)} %get-tuple-element.9.alpha_in, f32[16,64]{1,0:T(8,128)S(1)} %get-tuple-element.10.ga_in, f32[16,256]{1,0:T(8,128)S(1)} %get-tuple-element.11.gb_in), custom_call_target="tpu_custom_call" | custom-call | tf_op jit(solution)/shard_map/finish/pallas_call | solution.py:333

commit v7 on v6

--- a/solution.py
+++ b/solution.py
@@ -14,7 +14,7 @@
 GELU_A = 0.044715
 MESH = pl.DeviceIdType.MESH
 BITS = (1, 2, 4, 8)
-STRIP = 32
+STRIP = 16
 NT = (((1,), (1,)), ((), ()))
 TN = (((0,), (0,)), ((), ()))
 

time: 41.1 us -> 41.1 us (level)
  no operation moved by 1% of the time
where the time goes in v7:
time: 41.1 us; the launch traced here: 41 us
  Pallas kernels  40.4 us (98%)
  between operations  0.64 us (2%)
    pallas_call x1, Pallas kernels, device_step(): pl.pallas_call(functools.partial(kernel, (n_dev, tok * n_dev)), out_shape...  39.8 us

profile of v7, /device:TPU:0, one launch (start us, length us, event | category | flops | bytes accessed | tf_op | source)
XLA Modules:
  0.0 41.0 jit_solution(10240012567363869018)
XLA Ops:
  0.6 39.8 %step.1 = (f32[1,2]{1,0:T(1,128)S(1)}, f32[16,64]{1,0:T(8,128)S(1)}, f32[16,256]{1,0:T(8,128)S(1)}) custom-call(bf16[512,1024]{1,0:T(8,128)(2,1)} %x_hbm.1, s32[2,512]{1,0:T(2,128)} %lab_hbm.1, bf16[1024,4096]{1,0:T(8,128)(2,1)} %w1_hbm.1, bf16[4096,1024]{1,0:T(8,128)(2,1)} %w2_hbm.1, bf16[16,1024]{1,0:T(8,128)(2,1)} %bitcast.5, bf16[16,4096]{1,0:T(8,128)(2,1)} %b_hbm.1, ...), custom_call_target="tpu_custom_call" | custom-call | tf_op jit(solution)/shard_map/step/pallas_call | solution.py:294
  40.4 0.6 %finish.1 = (f32[1,2]{1,0:T(1,128)}, f32[16,64]{1,0:T(8,128)}, f32[16,256]{1,0:T(8,128)}) custom-call(f32[1,2]{1,0:T(1,128)S(1)} %get-tuple-element.9.alpha_in, f32[16,64]{1,0:T(8,128)S(1)} %get-tuple-element.10.ga_in, f32[16,256]{1,0:T(8,128)S(1)} %get-tuple-element.11.gb_in), custom_call_target="tpu_custom_call" | custom-call | tf_op jit(solution)/shard_map/finish/pallas_call | solution.py:333
